TPU v7x, 32 devices: a whole 2x2x4 slice. The times are simulated.
32 devices in a mesh: row: 4 (over z), col: 8 (over y, x, core).
Axes of the slice: x: 2, y: 2, z: 4, core: 2. Of those that a mesh axis runs over, the one named last changes fastest.
Arguments:
- factor_wide: float32 [4, 4, 2, 8, 512, 512], P(None, 'row', None, 'col'), may hold values from -1 to 2, as said below
- factor_narrow: bfloat16 [4, 4, 2, 8, 512, 512], P(None, 'row', None, 'col'), may hold values from -1 to 2, as said below
- flags: int32 [4, 4, 2, 8], P(None, 'row', None, 'col'), may hold values from 0 to 1
- forward_solution: float32 [2, 8, 512, 128], P(None, 'col'), may hold values from -0.5 to 0.5
- solution_grad: float32 [2, 8, 512, 128], P(None, 'col'), may hold values from -1.8 to 1.8
Outputs:
- rhs_grad: float32 [4, 4, 512, 128], P(None, 'row')
- factor_grad: float32 [4, 4, 2, 8, 512, 512], P(None, 'row', None, 'col')
Inputs may be any that keep to these rules, and one draw needn't show every extreme that they name: `factor_wide`: the diagonal entries of every diagonal tile lie between 1 and 2. `factor_narrow`: the diagonal entries of every diagonal tile lie between 1 and 2.
All inputs are finite; a program needn't handle non-finite values.
Results may differ from a plain program's by a relative error of at most 0.0003.
Values sent between devices are 32-bit elements; how exact they have to be, the bound alone decides.
A program may use at most 64 MiB of HBM per device.

v0:
```python
import functools

import jax
import jax.numpy as jnp
from jax import lax
from jax.experimental import pallas as pl
from jax.experimental.pallas import tpu as pltpu
from jax.sharding import PartitionSpec as P

HIGHEST_PRECISION = lax.Precision.HIGHEST
PRODUCT_PRECISION = lax.Precision.HIGH
BASE_BLOCK = 128
MESH = pl.DeviceIdType.MESH


def lower_mask(row_index, col_index, tile_width):
    inner_mask = lax.broadcasted_iota(
        jnp.int32, (tile_width, tile_width), 0
    ) >= lax.broadcasted_iota(jnp.int32, (tile_width, tile_width), 1)
    return (row_index > col_index) | (row_index == col_index) & inner_mask


def matmul(a, b):
    return jnp.dot(a, b, precision=HIGHEST_PRECISION, preferred_element_type=jnp.float32)


def split(value):
    high = value.astype(jnp.bfloat16)
    return high, (value - high.astype(jnp.float32)).astype(jnp.bfloat16)


def split_product(value, high, low):
    count = value.shape[0]
    value_high, value_low = split(value)
    both = jnp.concatenate([value_high, value_low], axis=0)
    first = jnp.dot(both, high, preferred_element_type=jnp.float32)
    second = jnp.dot(value_high, low, preferred_element_type=jnp.float32)
    return first[:count] + (first[count:] + second)


def invert_kernel(tile_ref, inverse_ref):
    width = tile_ref.shape[0]
    base = min(BASE_BLOCK, width)
    row = lax.broadcasted_iota(jnp.int32, (base, base), 0)
    col = lax.broadcasted_iota(jnp.int32, (base, base), 1)
    starts = range(0, width, base)
    blocks = [tile_ref[at:at + base, at:at + base] for at in starts]
    inverses = [jnp.where(row == col, 1.0 / jnp.where(row == col, b, 1.0), 0.0) for b in blocks]
    size = 1
    while size < base:
        corner = (row // (2 * size) == col // (2 * size)) & (row // size > col // size)
        halves = [matmul(x, jnp.where(corner, b, 0.0)) for x, b in zip(inverses, blocks)]
        inverses = [x - matmul(h, x) for x, h in zip(inverses, halves)]
        size *= 2
    inverse_ref[...] = jnp.zeros((width, width), jnp.float32)
    for at, x in zip(starts, inverses):
        inverse_ref[at:at + base, at:at + base] = x
    while size < width:
        for at in range(0, width, 2 * size):
            top, low = slice(at, at + size), slice(at + size, at + 2 * size)
            half = matmul(inverse_ref[low, low], tile_ref[low, top])
            inverse_ref[low, top] = -matmul(half, inverse_ref[top, top])
        size *= 2


def invert(tile):
    return pl.pallas_call(
        invert_kernel, out_shape=jax.ShapeDtypeStruct(tile.shape, jnp.float32)
    )(tile)


def sweep_kernel(rows, cols, tiles_ref, target_ref, *refs):
    local_cols = tiles_ref.shape[1]
    inverse_refs, below_refs = refs[:local_cols], refs[local_cols:2 * local_cols]
    (
        solved_ref, chain, total, parts, weights, chain_send, plane_send, part_send,
        chain_recv, plane_recv, part_recv,
    ) = refs[2 * local_cols:]
    my_row, my_col = lax.axis_index("row"), lax.axis_index("col")
    local_rows = tiles_ref.shape[0]
    count = local_rows * rows
    gaps = [d for d in range(2, rows + 2) if d != rows]

    def away(row_step, col_step):
        return (lax.rem(my_row + row_step + rows, rows), lax.rem(my_col + col_step + cols, cols))

    partners = [away(0, o) for o in range(1, cols)] + [away(o, 0) for o in range(1, rows)]
    partners += [away(1, 1), away(-1, -1)]
    barrier = pltpu.get_barrier_semaphore()
    for partner in partners:
        pl.semaphore_signal(barrier, inc=1, device_id=partner, device_id_type=MESH)
    pl.semaphore_wait(barrier, len(partners))

    total[...] = jnp.zeros_like(total)
    for s in range(local_cols):
        weights[s, 0], weights[s, 1] = split(inverse_refs[s][...])
        weights[s, 2], weights[s, 3] = split(below_refs[s][...])

    def chain_copy(slot, landing):
        return pltpu.make_async_remote_copy(
            src_ref=solved_ref.at[slot], dst_ref=chain.at[landing],
            send_sem=chain_send.at[slot], recv_sem=chain_recv.at[landing],
            device_id=away(-1, -1), device_id_type=MESH,
        )

    def plane_copy(slot, offset):
        return pltpu.make_async_remote_copy(
            src_ref=solved_ref.at[slot], dst_ref=solved_ref.at[slot],
            send_sem=plane_send.at[slot, offset], recv_sem=plane_recv.at[slot],
            device_id=away(0, -offset), device_id_type=MESH,
        )

    def part_copy(slot, where, gap):
        return pltpu.make_async_remote_copy(
            src_ref=total.at[slot], dst_ref=parts.at[slot, where],
            send_sem=part_send.at[slot], recv_sem=part_recv.at[slot, where],
            device_id=away((-gap) % rows, 0), device_id_type=MESH,
        )

    plane_order = list(range(2, cols)) + [1]

    def step(offset, carry):
        j = count - 1 - offset
        slot, col_slot = j // rows, j // cols
        on_plane = my_row == lax.rem(j, rows)
        owner = on_plane & (my_col == lax.rem(j, cols))

        @pl.when(owner)
        def _():
            total[col_slot] = target_ref[col_slot] - total[col_slot]
            for where, gap in enumerate(gaps):
                @pl.when(j + gap < count)
                def _():
                    part_copy(col_slot, where, gap).wait_recv()
                    total[col_slot] = total[col_slot] - parts[col_slot, where]
            solved_ref[slot] = split_product(
                total[col_slot], weights[col_slot, 0], weights[col_slot, 1]
            )

            @pl.when(j + 1 < count)
            def _():
                chain_copy(slot, col_slot).wait_recv()
                solved_ref[slot] = solved_ref[slot] - split_product(
                    chain[col_slot], weights[col_slot, 2], weights[col_slot, 3]
                )

            @pl.when(j > 0)
            def _():
                chain_copy(slot, (j - 1) // cols).start()
            for o in plane_order:
                plane_copy(slot, o).start()

        @pl.when(on_plane & jnp.logical_not(owner))
        def _():
            plane_copy(slot, 1).wait_recv()

        @pl.when(on_plane)
        def _():
            for s in reversed(range(local_cols)):
                k = my_col + cols * s

                @pl.when(k < j - 1)
                def _():
                    total[s] = total[s] + split_product(
                        solved_ref[slot], *split(tiles_ref[slot, s])
                    )
                for where, gap in enumerate(gaps):
                    @pl.when(k == j - gap)
                    def _():
                        part_copy(s, where, gap).start()
        return carry

    lax.fori_loop(0, count, step, 0)

    def drain(offset, carry):
        j = count - 1 - offset
        slot = j // rows
        on_plane = my_row == lax.rem(j, rows)

        @pl.when(on_plane & (my_col == lax.rem(j, cols)))
        def _():
            @pl.when(j > 0)
            def _():
                chain_copy(slot, 0).wait_send()
            for o in plane_order:
                plane_copy(slot, o).wait_send()

        @pl.when(on_plane)
        def _():
            for s in range(local_cols):
                for where, gap in enumerate(gaps):
                    @pl.when(my_col + cols * s == j - gap)
                    def _():
                        part_copy(s, where, gap).wait_send()
        return carry

    lax.fori_loop(0, count, drain, 0)


def sweep(rows, cols, tiles, target, inverses, corrections):
    local_rows, local_cols, width = tiles.shape[0], tiles.shape[1], tiles.shape[2]
    rhs = target.shape[1]
    vmem = pl.BlockSpec(memory_space=pltpu.VMEM)
    dma = pltpu.SemaphoreType.DMA
    return pl.pallas_call(
        functools.partial(sweep_kernel, rows, cols),
        out_shape=jax.ShapeDtypeStruct((local_rows, rhs, width), jnp.float32),
        in_specs=[vmem] * (2 + 2 * local_cols),
        out_specs=vmem,
        scratch_shapes=[
            pltpu.VMEM((local_cols, rhs, width), jnp.float32),
            pltpu.VMEM((local_cols, rhs, width), jnp.float32),
            pltpu.VMEM((local_cols, rows - 1, rhs, width), jnp.float32),
            pltpu.VMEM((local_cols, 4, width, width), jnp.bfloat16),
            dma((local_rows,)),
            dma((local_rows, cols)),
            dma((local_cols,)),
            dma((local_cols,)),
            dma((local_rows,)),
            dma((local_cols, rows - 1)),
        ],
        compiler_params=pltpu.CompilerParams(collective_id=0, has_side_effects=True),
    )(tiles, target, *inverses, *corrections)


def body(factor_wide, factor_narrow, flags, forward_solution, solution_grad):
    row_count = lax.axis_size("row")
    col_count = lax.axis_size("col")
    my_row = lax.axis_index("row")
    my_col = lax.axis_index("col")
    local_rows = factor_wide.shape[0]
    local_cols = factor_wide.shape[2]
    tile_width = factor_wide.shape[4]
    tile_count = local_rows * row_count

    def pick(row_slot, col_slot):
        def cut(pool):
            return lax.dynamic_index_in_dim(pool[:, 0, col_slot, 0], row_slot, 0, keepdims=False)
        narrow = cut(flags) == 1
        return jnp.where(narrow, cut(factor_narrow).astype(jnp.float32), cut(factor_wide))

    targets = [my_col + col_count * s for s in range(local_cols)]
    holders = [
        (r, c) for r in range(row_count) for c in range(col_count)
        if any((c + col_count * s) % row_count == r for s in range(local_cols))
    ]
    to_holders = [
        ((r + 1) % row_count * col_count + c, r * col_count + c) for r, c in holders
    ]
    below = [None] * local_cols
    for s in reversed(range(local_cols)):
        tile = pick(jnp.minimum(targets[s] + 1, tile_count - 1) // row_count, s)
        below[s] = lax.ppermute(tile, ("row", "col"), to_holders)
    factor_tiles = jnp.where(
        flags[:, 0, :, 0, None, None] == 1,
        factor_narrow[:, 0, :, 0].astype(jnp.float32),
        factor_wide[:, 0, :, 0],
    )
    inverses = [invert(pick(j // row_count, s)) for s, j in enumerate(targets)]
    corrections = [
        jnp.dot(b, v, precision=PRODUCT_PRECISION, preferred_element_type=jnp.float32)
        for b, v in zip(below, inverses)
    ]
    target = jnp.swapaxes(solution_grad[:, 0], 1, 2)
    solved = sweep(row_count, col_count, factor_tiles, target, inverses, corrections)
    row_index = jnp.arange(local_rows, dtype=jnp.int32) * row_count + my_row
    col_index = jnp.arange(local_cols, dtype=jnp.int32) * col_count + my_col
    products = -jnp.einsum(
        "ark,blr->abkl", solved, forward_solution[:, 0], precision=PRODUCT_PRECISION
    )
    masks = lower_mask(row_index[:, None, None, None], col_index[None, :, None, None], tile_width)
    factor_grad = jnp.where(masks, products, jnp.zeros_like(products))
    return (jnp.swapaxes(solved, 1, 2)[:, None], factor_grad[:, None, :, None])


def solution(mesh):
    placed = (
        P(None, "row", None, "col", None, None),
        P(None, "row", None, "col", None, None),
        P(None, "row", None, "col"),
        P(None, "col", None, None),
        P(None, "col", None, None),
    )
    return jax.shard_map(
        body,
        mesh=mesh,
        in_specs=placed,
        out_specs=(P(None, "row", None, None), P(None, "row", None, "col", None, None)),
        check_vma=False,
    )
```

profile of v0, /device:TPU:2, one launch (start us, length us, event | category | flops | bytes accessed | tf_op | source)
XLA Modules:
  0.0 188.4 jit_solution(9182023918760422102)
XLA Ops:
  0.6 0.0 copy-start
  0.7 0.7 fusion.5
  1.4 0.7 constant_dynamic-slice_fusion
  3.3 0.0 copy-start.1
  3.3 4.7 %fusion.3 = (f32[4,1,1,1,512,512]{5,4,3,2,1,0:T(8,128)S(1)}, f32[4,1,1,1,512,512]{5,4,3,2,1,0:T(8,128)S(1)}) fusion(f32[4,1,2,1,512,512]{5,4,3,2,1,0:T(8,128)} %param.5), kind=kLoop, calls=%fused_computation.19 | loop fusion | bytes 16777216 | tf_op jit(solution)/shard_map/slice | solution.py:238
  8.0 0.0 copy-done.1
  8.0 0.5 fusion.4
  8.5 0.0 copy-start.5
  8.5 1.7 select_bitcast_fusion
  10.2 1.7 collective-permute-start.1
  13.1 0.0 copy-start.4
  13.1 1.7 select_bitcast_fusion.1
  14.8 1.6 collective-permute-start
  16.4 0.0 copy-done.5
  16.4 0.1 iota_compare_fusion
  16.5 7.0 %shard_map.69.refs_1_ = f32[512,512]{1,0:T(8,128)} custom-call(f32[512,512]{1,0:T(8,128)} %get-tuple-element.7.tile_ref), custom_call_target="tpu_custom_call" | custom-call | tf_op jit(solution)/shard_map/pallas_call | solution.py:67
  23.5 6.9 %shard_map.68.refs_0_ = f32[512,512]{1,0:T(8,128)} custom-call(f32[512,512]{1,0:T(8,128)} %get-tuple-element.9.tile_ref), custom_call_target="tpu_custom_call" | custom-call | tf_op jit(solution)/shard_map/pallas_call | solution.py:67
  30.4 0.1 copy.7
  30.5 0.0 copy-done.4
  30.5 1.0 copy.9
  31.6 0.1 broadcast_compare_fusion.1
  31.6 9.8 %convert_select_fusion.tiles_ref = f32[4,2,512,512]{3,2,1,0:T(8,128)} fusion(f32[4,1,2,1,512,512]{5,4,3,2,1,0:T(8,128)} %param.5, bf16[4,1,2,1,512,512]{5,4,3,2,1,0:T(8,128)(2,1)} %param.6, pred[4,2]{1,0:T(4,128)(4,1)S(1)} %bitcast.49), kind=kLoop, calls=%fused_computation | loop fusion | flops 4194304 | bytes 20971528 | tf_op jit(solution)/shard_map/jit(_where)/select_n | solution.py:254
  41.4 0.0 collective-permute-done.1
  41.4 0.0 copy-done.2
  41.4 3.2 %fusion.7.refs_3_ = f32[512,512]{1,0:T(8,128)} fusion(f32[512,512]{1,0:T(8,128)} %collective-permute-done.1, f32[512,512]{1,0:T(8,128)S(1)} %copy-done.2), kind=kOutput, calls=%fused_computation.23 | convolution fusion | flops 805306368 | bytes 3145728 | tf_op jit(solution)/shard_map/dot_general | solution.py:261
  44.6 0.0 collective-permute-done
  44.6 0.0 copy-done.3
  44.6 3.4 %fusion.6.refs_2_ = f32[512,512]{1,0:T(8,128)} fusion(f32[512,512]{1,0:T(8,128)} %collective-permute-done, f32[512,512]{1,0:T(8,128)S(1)} %copy-done.3), kind=kOutput, calls=%fused_computation.22 | convolution fusion | flops 805306368 | bytes 3145728 | tf_op jit(solution)/shard_map/dot_general | solution.py:261
  48.1 127.8 %shard_map.70 = f32[4,128,512]{2,1,0:T(8,128)} custom-call(f32[4,2,512,512]{3,2,1,0:T(8,128)} %convert_select_fusion.tiles_ref, f32[2,128,512]{2,1,0:T(8,128)} %bitcast.48, f32[512,512]{1,0:T(8,128)} %shard_map.68.refs_0_, f32[512,512]{1,0:T(8,128)} %shard_map.69.refs_1_, f32[512,512]{1,0:T(8,128)} %fusion.6.refs_2_, f32[512,512]{1,0:T(8,128)} %fusion.7.refs_3_), custom_call_target="tpu_custom_call" | custom-call | tf_op jit(solution)/shard_map/pallas_call | solution.py:205
  175.9 2.5 %copy.11 = f32[4,1,512,128]{3,2,1,0:T(8,128)} copy(f32[4,1,512,128]{2,3,0,1:T(8,128)} %bitcast.47) | data formatting | bytes 2097152
  178.4 0.0 copy-done
  178.4 9.9 %fusion = f32[4,1,2,1,512,512]{5,4,3,2,1,0:T(8,128)} fusion(pred[512,512]{1,0:T(8,128)(4,1)S(1)} %iota_compare_fusion, pred[4,2]{1,0:T(4,128)(4,1)S(1)} %get-tuple-element.13, pred[4,2]{1,0:T(4,128)(4,1)S(1)} %get-tuple-element.12, f32[4,128,512]{2,1,0:T(8,128)} %shard_map.70, f32[2,1,512,128]{3,2,1,0:T(8,128)S(1)} %copy-done), kind=kOutput, calls=%fused_computation.2 | convolution fusion | flops 1619001344 | bytes 10223632 | tf_op jit(solution)/shard_map/ark,blr->abkl/dot_general | solution.py:268
  (5 shorter events, 0.0 us)
Async XLA Ops:
  0.6 177.8 %copy-start = (f32[2,1,512,128]{3,2,1,0:T(8,128)S(1)}, f32[2,1,512,128]{3,2,1,0:T(8,128)}, u32[]{:S(2)}) copy-start(f32[2,1,512,128]{3,2,1,0:T(8,128)} %param.8) | copy-start | bytes 1572868
  3.3 4.7 %copy-start.1 = (bf16[4,1,2,1,512,512]{5,4,3,2,1,0:T(8,128)(2,1)S(1)}, bf16[4,1,2,1,512,512]{5,4,3,2,1,0:T(8,128)(2,1)}, u32[]{:S(2)}) copy-start(bf16[4,1,2,1,512,512]{5,4,3,2,1,0:T(8,128)(2,1)} %param.6) | copy-start | bytes 12582916
  8.5 7.9 %copy-start.5 = (s32[4,1,2,1]{0,3,2,1:T(1,128)S(1)}, s32[4,1,2,1]{0,3,2,1:T(1,128)}, u32[]{:S(2)}) copy-start(s32[4,1,2,1]{0,3,2,1:T(1,128)} %param.7) | copy-start | bytes 100
  10.2 31.2 %collective-permute-start.1 = (f32[512,512]{1,0:T(8,128)}, f32[512,512]{1,0:T(8,128)}, u32[]{:S(2)}, u32[]{:S(2)}) collective-permute-start(f32[512,512]{1,0:T(8,128)} %get-tuple-element.6), channel_id=1, source_target_pairs={{8,0},{12,4},{17,9},{21,13},{26,18},{30,22},{3,27},{7,31}} | collective-permute-start | bytes 3145736 | tf_op jit(solution)/shard_map/ppermute | solution.py:253
  13.1 17.4 %copy-start.4 = (f32[2,1,512,128]{3,2,1,0:T(8,128)S(1)}, f32[2,1,512,128]{3,2,1,0:T(8,128)}, u32[]{:S(2)}) copy-start(f32[2,1,512,128]{3,2,1,0:T(8,128)} %param.9) | copy-start | bytes 1572868
  14.8 29.8 %collective-permute-start = (f32[512,512]{1,0:T(8,128)}, f32[512,512]{1,0:T(8,128)}, u32[]{:S(2)}, u32[]{:S(2)}) collective-permute-start(f32[512,512]{1,0:T(8,128)} %get-tuple-element.8), channel_id=1, source_target_pairs={{8,0},{12,4},{17,9},{21,13},{26,18},{30,22},{3,27},{7,31}} | collective-permute-start | bytes 3145736 | tf_op jit(solution)/shard_map/ppermute | solution.py:253
  31.6 9.8 %copy-start.2 = (f32[512,512]{1,0:T(8,128)S(1)}, f32[512,512]{1,0:T(8,128)}, u32[]{:S(2)}) copy-start(f32[512,512]{1,0:T(8,128)} %shard_map.69.refs_1_) | copy-start | bytes 3145732
  31.6 13.0 %copy-start.3 = (f32[512,512]{1,0:T(8,128)S(1)}, f32[512,512]{1,0:T(8,128)}, u32[]{:S(2)}) copy-start(f32[512,512]{1,0:T(8,128)} %shard_map.68.refs_0_) | copy-start | bytes 3145732
where the time goes:
time: 192 us; the launch traced here: 188 us
  Pallas kernels  142 us (74%)
  matrix products  16.6 us (9%)
  other arithmetic  13.3 us (7%)
  local copies, waits for them, and re-layouts  10.2 us (5%)
  between operations  3.31 us (2%)
  starting transfers between devices  3.29 us (2%)
    pallas_call x1, Pallas kernels, sweep(): pl.pallas_call(functools.partial(sweep_kernel, rows, cols), out_shape=jax...  128 us
    pallas_call x2, Pallas kernels, invert(): pl.pallas_call(invert_kernel, out_shape=jax.ShapeDtypeStruct(tile.shape,...  13.9 us
    dot_general x1, matrix products, body(): jnp.einsum('ark,blr->abkl', solved, forward_solution[:, 0], precision=PRO...  9.91 us
    select_n x1, other arithmetic, body(): jnp.where(flags[:, 0, :, 0, None, None] == 1, factor_narrow[:, 0, :, 0].a...  9.76 us
    dot_general x2, matrix products, body(): jnp.dot(b, v, precision=PRODUCT_PRECISION, preferred_element_type=jnp.flo...  6.66 us
    slice x3, local copies, waits for them, and re-layouts, cut(): pool[:, 0, col_slot, 0]  5.86 us
  transfers between devices with their start and end apart: 2, of which 0 were waited for; matrix products, arithmetic and copies ran while one was open for 8% of the time, Pallas kernels for 7%

commit v1 on v0

v1 whole, which is shorter than its diff:
```python
import functools

import jax
import jax.numpy as jnp
from jax import lax
from jax.experimental import pallas as pl
from jax.experimental.pallas import tpu as pltpu
from jax.sharding import PartitionSpec as P

BASE_BLOCK = 128
CHUNKS = 4
MESH = pl.DeviceIdType.MESH
VMEM_LIMIT = 60 * 1024 * 1024


def split(value):
    high = value.astype(jnp.bfloat16)
    return high, (value - high.astype(jnp.float32)).astype(jnp.bfloat16)


def split_product(value, high, low):
    count = value.shape[0]
    value_high, value_low = split(value)
    both = jnp.concatenate([value_high, value_low], axis=0)
    first = jnp.dot(both, high, preferred_element_type=jnp.float32)
    second = jnp.dot(value_high, low, preferred_element_type=jnp.float32)
    return first[:count] + (first[count:] + second)


def product(a, b):
    a_high, a_low = split(a)
    b_high, b_low = split(b)
    left = jnp.concatenate([a_high, a_low, a_high], axis=1)
    right = jnp.concatenate([b_high, b_high, b_low], axis=0)
    return jnp.dot(left, right, preferred_element_type=jnp.float32)


def invert(tile_ref, inverse_ref):
    width = tile_ref.shape[0]
    base = min(BASE_BLOCK, width)
    row = lax.broadcasted_iota(jnp.int32, (base, base), 0)
    col = lax.broadcasted_iota(jnp.int32, (base, base), 1)
    starts = range(0, width, base)
    blocks = [tile_ref[at:at + base, at:at + base] for at in starts]
    inverses = [jnp.where(row == col, 1.0 / jnp.where(row == col, b, 1.0), 0.0) for b in blocks]
    size = 1
    while size < base:
        corner = (row // (2 * size) == col // (2 * size)) & (row // size > col // size)
        halves = [product(x, jnp.where(corner, b, 0.0)) for x, b in zip(inverses, blocks)]
        inverses = [x - product(h, x) for x, h in zip(inverses, halves)]
        size *= 2
    inverse_ref[...] = jnp.zeros((width, width), jnp.float32)
    for at, x in zip(starts, inverses):
        inverse_ref[at:at + base, at:at + base] = x
    while size < width:
        for at in range(0, width, 2 * size):
            top, low = slice(at, at + size), slice(at + size, at + 2 * size)
            half = product(inverse_ref[low, low], tile_ref[low, top])
            inverse_ref[low, top] = -product(half, inverse_ref[top, top])
        size *= 2


def sweep_kernel(
    rows, cols, wide_ref, narrow_ref, flags_ref, target_ref, solved_ref,
    tiles, narrows, total, chain, parts, below, inverse, weights, pairs,
    load_sem, chain_send, chain_recv, plane_send, plane_recv,
    part_send, part_recv, below_send, below_recv,
):
    my_row, my_col = lax.axis_index("row"), lax.axis_index("col")
    local_rows, local_cols = tiles.shape[0], tiles.shape[1]
    rhs, width = total.shape[1], total.shape[2]
    chunk = rhs // CHUNKS
    count = local_rows * rows
    gaps = [d for d in range(2, rows + 2) if d != rows]
    urgent = [d for d in (2, 3) if d in gaps and d < cols]
    calm = [o for o in range(2, cols) if o not in urgent] + [1]

    def away(row_step, col_step):
        return (lax.rem(my_row + row_step + rows, rows), lax.rem(my_col + col_step + cols, cols))

    def target_of(s):
        return my_col + cols * s

    def owns(s):
        return lax.rem(target_of(s), rows) == my_row

    def loads(a, s):
        return (
            pltpu.make_async_copy(wide_ref.at[a, 0, s, 0], tiles.at[a, s], load_sem.at[a, s, 0]),
            pltpu.make_async_copy(narrow_ref.at[a, 0, s, 0], narrows.at[a, s], load_sem.at[a, s, 1]),
        )

    def start_loads(s):
        for a in reversed(range(local_rows)):
            @pl.when(a * rows + my_row >= target_of(s))
            def _():
                for copy in loads(a, s):
                    copy.start()

    def tile_value(a, s, at, size):
        flag = jnp.full((size, width), flags_ref[a, 0, s, 0], jnp.int32)
        narrow = narrows[a, s, pl.ds(at, size), :].astype(jnp.float32)
        return jnp.where(flag == 1, narrow, tiles[a, s, pl.ds(at, size), :])

    def settle(a, s, use):
        for copy in loads(a, s):
            copy.wait()
        size = min(128, width)

        def piece(p, carry):
            at = pl.multiple_of(p * size, size)
            use(at, size, tile_value(a, s, at, size))
            return carry

        lax.fori_loop(0, width // size, piece, 0)

    def settle_in_place(a, s):
        def use(at, size, value):
            tiles[a, s, pl.ds(at, size), :] = value
        settle(a, s, use)

    def settle_pair(a, s):
        def use(at, size, value):
            high, low = split(value)
            pairs[s, 0, pl.ds(at, size), :] = high
            pairs[s, 1, pl.ds(at, size), :] = low
        settle(a, s, use)

    def span(c):
        return pl.ds(pl.multiple_of(c * chunk, chunk), chunk)

    def chain_copy(slot, landing, c):
        return pltpu.make_async_remote_copy(
            src_ref=solved_ref.at[slot, span(c)], dst_ref=chain.at[landing, span(c)],
            send_sem=chain_send.at[slot, c], recv_sem=chain_recv.at[landing, c],
            device_id=away(-1, -1), device_id_type=MESH,
        )

    def plane_chunk(slot, offset, c):
        return pltpu.make_async_remote_copy(
            src_ref=solved_ref.at[slot, span(c)], dst_ref=solved_ref.at[slot, span(c)],
            send_sem=plane_send.at[slot, offset, c], recv_sem=plane_recv.at[slot, c],
            device_id=away(0, -offset), device_id_type=MESH,
        )

    def plane_whole(slot, offset):
        return pltpu.make_async_remote_copy(
            src_ref=solved_ref.at[slot], dst_ref=solved_ref.at[slot],
            send_sem=plane_send.at[slot, offset, 0], recv_sem=plane_recv.at[slot, 0],
            device_id=away(0, -offset), device_id_type=MESH,
        )

    def part_copy(slot, where, gap, c):
        return pltpu.make_async_remote_copy(
            src_ref=total.at[slot, span(c)], dst_ref=parts.at[slot, where, span(c)],
            send_sem=part_send.at[slot, c], recv_sem=part_recv.at[slot, where, c],
            device_id=away((-gap) % rows, 0), device_id_type=MESH,
        )

    def below_copy(a, s):
        return pltpu.make_async_remote_copy(
            src_ref=tiles.at[a, s], dst_ref=below.at[s],
            send_sem=below_send.at[s], recv_sem=below_recv.at[s],
            device_id=away(-1, 0), device_id_type=MESH,
        )

    def ships(s):
        return (lax.rem(target_of(s) + 1, rows) == my_row) & (target_of(s) + 1 < count)

    start_loads(local_cols - 1)
    partners = [away(0, o) for o in range(1, cols)] + [away(o, 0) for o in range(1, rows)]
    partners += [away(1, 1), away(-1, -1)]
    barrier = pltpu.get_barrier_semaphore()
    for partner in partners:
        pl.semaphore_signal(barrier, inc=1, device_id=partner, device_id_type=MESH)
    pl.semaphore_wait(barrier, len(partners))
    for s in reversed(range(local_cols - 1)):
        start_loads(s)

    for s in reversed(range(local_cols)):
        @pl.when(ships(s))
        def _():
            a = (target_of(s) + 1) // rows
            settle_in_place(a, s)
            below_copy(a, s).start()

    for s in range(local_cols):
        @pl.when(owns(s))
        def _():
            total[s] = target_ref[s, 0].T

        @pl.when(jnp.logical_not(owns(s)))
        def _():
            total[s] = jnp.zeros((rhs, width), jnp.float32)

    def prepare(s):
        k = target_of(s)
        settle_in_place(k // rows, s)
        invert(tiles.at[k // rows, s], inverse)
        size = min(128, width)

        def store(at, first, value):
            high, low = split(value)
            weights[s, first, pl.ds(at, size), :] = high
            weights[s, first + 1, pl.ds(at, size), :] = low

        def keep(p, carry):
            at = pl.multiple_of(p * size, size)
            store(at, 0, inverse[pl.ds(at, size), :])
            return carry

        lax.fori_loop(0, width // size, keep, 0)

        @pl.when(k + 1 < count)
        def _():
            below_copy(0, s).wait_recv()

            def correct(p, carry):
                at = pl.multiple_of(p * size, size)
                store(at, 2, split_product(below[s, pl.ds(at, size), :], weights[s, 0], weights[s, 1]))
                return carry

            lax.fori_loop(0, width // size, correct, 0)

    def accumulate(slot, s, where):
        total[s, where] = total[s, where] - split_product(
            solved_ref[slot, where], pairs[s, 0], pairs[s, 1]
        )

    def step(own_slot, j):
        slot = j // rows
        on_plane = my_row == lax.rem(j, rows)
        offset = lax.rem(lax.rem(j, cols) - my_col + cols, cols)
        owner = on_plane & (offset == 0)

        @pl.when(owner)
        def _():
            def solve(c, carry):
                here = span(c)
                for where, gap in reversed(list(enumerate(gaps))):
                    @pl.when(j + gap < count)
                    def _():
                        part_copy(own_slot, where, gap, c).wait_recv()
                        total[own_slot, here] = total[own_slot, here] + parts[own_slot, where, here]
                solved_ref[slot, here] = split_product(
                    total[own_slot, here], weights[own_slot, 0], weights[own_slot, 1]
                )

                @pl.when(j + 1 < count)
                def _():
                    chain_copy(slot, own_slot, c).wait_recv()
                    solved_ref[slot, here] = solved_ref[slot, here] - split_product(
                        chain[own_slot, here], weights[own_slot, 2], weights[own_slot, 3]
                    )

                @pl.when(j > 0)
                def _():
                    chain_copy(slot, (j - 1) // cols, c).start()
                for o in urgent:
                    plane_chunk(slot, o, c).start()
                return carry

            lax.fori_loop(0, CHUNKS, solve, 0)
            for o in calm:
                plane_whole(slot, o).start()

        @pl.when(on_plane)
        def _():
            for s in reversed(range(local_cols)):
                @pl.when(target_of(s) < j - 1)
                def _():
                    settle_pair(slot, s)

        is_urgent = on_plane & functools.reduce(
            jnp.logical_or, [offset == o for o in urgent], jnp.bool_(False)
        )

        @pl.when(is_urgent)
        def _():
            k = j - offset

            def follow(c, carry):
                plane_chunk(slot, 1, c).wait_recv()

                @pl.when(k >= 0)
                def _():
                    s = k // cols
                    accumulate(slot, s, span(c))
                    for where, gap in enumerate(gaps):
                        if gap in urgent:
                            @pl.when(offset == gap)
                            def _():
                                part_copy(s, where, gap, c).start()
                return carry

            lax.fori_loop(0, CHUNKS, follow, 0)

        @pl.when(on_plane & jnp.logical_not(is_urgent) & jnp.logical_not(owner))
        def _():
            plane_whole(slot, 1).wait_recv()

        @pl.when(on_plane)
        def _():
            for s in reversed(range(local_cols)):
                k = target_of(s)

                @pl.when((k < j - 1) & jnp.logical_not(is_urgent & (k == j - offset)))
                def _():
                    accumulate(slot, s, pl.ds(0, rhs))
                    for where, gap in enumerate(gaps):
                        if gap not in urgent:
                            @pl.when(k == j - gap)
                            def _():
                                for c in range(CHUNKS):
                                    part_copy(s, where, gap, c).start()

    def half(h, carry):
        own_slot = local_cols - 1 - h

        @pl.when(owns(own_slot))
        def _():
            prepare(own_slot)

        def one(o, inner):
            step(own_slot, (own_slot + 1) * cols - 1 - o)
            return inner

        return lax.fori_loop(0, cols, one, carry)

    lax.fori_loop(0, local_cols, half, 0)

    for s in reversed(range(local_cols)):
        @pl.when(ships(s))
        def _():
            below_copy(0, s).wait_send()

    def drain(i, carry):
        j = count - 1 - i
        slot = j // rows
        on_plane = my_row == lax.rem(j, rows)

        @pl.when(on_plane & (my_col == lax.rem(j, cols)))
        def _():
            def sent(c, inner):
                @pl.when(j > 0)
                def _():
                    chain_copy(slot, 0, c).wait_send()
                for o in urgent:
                    plane_chunk(slot, o, c).wait_send()
                return inner

            lax.fori_loop(0, CHUNKS, sent, 0)
            for o in calm:
                plane_whole(slot, o).wait_send()

        @pl.when(on_plane)
        def _():
            for s in range(local_cols):
                for where, gap in enumerate(gaps):
                    @pl.when(target_of(s) == j - gap)
                    def _():
                        for c in range(CHUNKS):
                            part_copy(s, where, gap, c).wait_send()
        return carry

    lax.fori_loop(0, count, drain, 0)


def sweep(rows, cols, wide, narrow, flags, target):
    local_rows, local_cols, width = wide.shape[0], wide.shape[2], wide.shape[4]
    rhs = target.shape[3]
    vmem = pl.BlockSpec(memory_space=pltpu.VMEM)
    hbm = pl.BlockSpec(memory_space=pl.ANY)
    dma = pltpu.SemaphoreType.DMA
    gaps = rows - 1
    return pl.pallas_call(
        functools.partial(sweep_kernel, rows, cols),
        out_shape=jax.ShapeDtypeStruct((local_rows, rhs, width), jnp.float32),
        in_specs=[hbm, hbm, pl.BlockSpec(memory_space=pltpu.SMEM), vmem],
        out_specs=vmem,
        scratch_shapes=[
            pltpu.VMEM((local_rows, local_cols, width, width), jnp.float32),
            pltpu.VMEM((local_rows, local_cols, width, width), jnp.bfloat16),
            pltpu.VMEM((local_cols, rhs, width), jnp.float32),
            pltpu.VMEM((local_cols, rhs, width), jnp.float32),
            pltpu.VMEM((local_cols, gaps, rhs, width), jnp.float32),
            pltpu.VMEM((local_cols, width, width), jnp.float32),
            pltpu.VMEM((width, width), jnp.float32),
            pltpu.VMEM((local_cols, 4, width, width), jnp.bfloat16),
            pltpu.VMEM((local_cols, 2, width, width), jnp.bfloat16),
            dma((local_rows, local_cols, 2)),
            dma((local_rows, CHUNKS)),
            dma((local_cols, CHUNKS)),
            dma((local_rows, cols, CHUNKS)),
            dma((local_rows, CHUNKS)),
            dma((local_cols, CHUNKS)),
            dma((local_cols, gaps, CHUNKS)),
            dma((local_cols,)),
            dma((local_cols,)),
        ],
        compiler_params=pltpu.CompilerParams(
            collective_id=0, has_side_effects=True, vmem_limit_bytes=VMEM_LIMIT
        ),
    )(wide, narrow, flags, target)


def finish_kernel(rows, cols, place_ref, solved_ref, x_ref, rhs_ref, grad_ref, left, right):
    a, s = pl.program_id(0), pl.program_id(1)
    local_cols, width = x_ref.shape[0], x_ref.shape[2]

    @pl.when((a == 0) & (s == 0))
    def _():
        for t in range(local_cols):
            high, low = split(x_ref[t, 0])
            right[t] = jnp.concatenate([high, high, low], axis=1)

    @pl.when(s == 0)
    def _():
        value = solved_ref[a].T
        rhs_ref[0, 0] = value
        high, low = split(-value)
        left[...] = jnp.concatenate([high, low, high], axis=1)

    i = a * rows + place_ref[0]
    k = s * cols + place_ref[1]

    def outer():
        return lax.dot_general(
            left[...], right[s], (((1,), (1,)), ((), ())), preferred_element_type=jnp.float32
        )

    @pl.when(i > k)
    def _():
        grad_ref[0, 0, 0, 0] = outer()

    @pl.when(i == k)
    def _():
        row = lax.broadcasted_iota(jnp.int32, (width, width), 0)
        col = lax.broadcasted_iota(jnp.int32, (width, width), 1)
        grad_ref[0, 0, 0, 0] = jnp.where(row >= col, outer(), 0.0)

    @pl.when(i < k)
    def _():
        grad_ref[0, 0, 0, 0] = jnp.zeros((width, width), jnp.float32)


def finish(rows, cols, place, solved, x):
    local_rows, rhs, width = solved.shape
    local_cols = x.shape[0]
    vmem = pl.BlockSpec(memory_space=pltpu.VMEM)
    return pl.pallas_call(
        functools.partial(finish_kernel, rows, cols),
        grid=(local_rows, local_cols),
        out_shape=(
            jax.ShapeDtypeStruct((local_rows, 1, width, rhs), jnp.float32),
            jax.ShapeDtypeStruct((local_rows, 1, local_cols, 1, width, width), jnp.float32),
        ),
        in_specs=[pl.BlockSpec(memory_space=pltpu.SMEM), vmem, vmem],
        out_specs=(
            pl.BlockSpec((1, 1, width, rhs), lambda a, s: (a, 0, 0, 0)),
            pl.BlockSpec((1, 1, 1, 1, width, width), lambda a, s: (a, 0, s, 0, 0, 0)),
        ),
        scratch_shapes=[
            pltpu.VMEM((width, 3 * rhs), jnp.bfloat16),
            pltpu.VMEM((local_cols, width, 3 * rhs), jnp.bfloat16),
        ],
    )(place, solved, x)


def body(factor_wide, factor_narrow, flags, forward_solution, solution_grad):
    rows, cols = lax.axis_size("row"), lax.axis_size("col")
    place = jnp.stack([lax.axis_index("row"), lax.axis_index("col")]).astype(jnp.int32)
    solved = sweep(rows, cols, factor_wide, factor_narrow, flags, solution_grad)
    return finish(rows, cols, place, solved, forward_solution)


def solution(mesh):
    placed = (
        P(None, "row", None, "col", None, None),
        P(None, "row", None, "col", None, None),
        P(None, "row", None, "col"),
        P(None, "col", None, None),
        P(None, "col", None, None),
    )
    return jax.shard_map(
        body,
        mesh=mesh,
        in_specs=placed,
        out_specs=(P(None, "row", None, None), P(None, "row", None, "col", None, None)),
        check_vma=False,
    )
```

time: 192 us -> 118 us (0.61)
  the two profiles are of different devices: /device:TPU:2 before, /device:TPU:0 now
where the time goes in v1:
time: 118 us; the launch traced here: 117 us
  Pallas kernels  115 us (97%)
  local copies, waits for them, and re-layouts  1.36 us (1%)
    pallas_call x1, Pallas kernels, sweep(): pl.pallas_call(functools.partial(sweep_kernel, rows, cols), out_shape=jax...  106 us
    pallas_call x1, Pallas kernels, finish(): pl.pallas_call(functools.partial(finish_kernel, rows, cols), grid=(local_...  8.51 us

profile of v1, /device:TPU:0, one launch (start us, length us, event | category | flops | bytes accessed | tf_op | source)
XLA Modules:
  0.0 117.4 jit_solution(14936494290809680091)
XLA Ops:
  0.6 0.7 pad_add_fusion.place_ref
  1.3 1.4 %copy.7.flags_ref = s32[4,1,2,1]{3,2,1,0:T(2,128)} copy(s32[4,1,2,1]{0,3,2,1:T(1,128)} %param.7) | data formatting | bytes 64 | tf_op args[2]
  2.7 106.2 %shard_map.68.solved_ref = f32[4,128,512]{2,1,0:T(8,128)} custom-call(f32[4,1,2,1,512,512]{5,4,3,2,1,0:T(8,128)} %wide_ref.1, bf16[4,1,2,1,512,512]{5,4,3,2,1,0:T(8,128)(2,1)} %narrow_ref.1, s32[4,1,2,1]{3,2,1,0:T(2,128)} %copy.7.flags_ref, f32[2,1,512,128]{3,2,1,0:T(8,128)} %target_ref.1), custom_call_target="tpu_custom_call" | custom-call | tf_op jit(solution)/shard_map/pallas_call | solution.py:376
  108.8 8.5 %shard_map.69 = (f32[4,1,512,128]{3,2,1,0:T(8,128)}, f32[4,1,2,1,512,512]{5,4,3,2,1,0:T(8,128)}) custom-call(s32[2]{0:T(128)} %pad_add_fusion.place_ref, f32[4,128,512]{2,1,0:T(8,128)} %shard_map.68.solved_ref, f32[2,1,512,128]{3,2,1,0:T(8,128)} %x_ref.1), custom_call_target="tpu_custom_call" | custom-call | tf_op jit(solution)/shard_map/pallas_call | solution.py:451
